TPU v7x, 32 devices: a whole 2x2x4 slice. The times are simulated.
32 devices in a mesh: tm: 16 (over z, x, core), tile: 2 (over y).
Axes of the slice: x: 2, y: 2, z: 4, core: 2. Of those that a mesh axis runs over, the one named last changes fastest.
Arguments:
- queries: bfloat16 [32, 4, 64, 2560], P('tm', 'tile'), may hold values from -40 to 40
- keys: bfloat16 [32, 4, 64, 2560], P('tm', 'tile'), may hold values from -6 to 6
- values: bfloat16 [32, 4, 64, 2560], P('tm', 'tile'), may hold values from -6 to 6
- neighbours: int32 [16, 2, 3], P('tm', 'tile'), may hold values from -1 to 14, as said below
- halo_rows: int32 [16, 2], P('tm', 'tile'), may hold values from 0 to 2, as said below
Outputs:
- attended: bfloat16 [32, 4, 64, 2560], P('tm', 'tile')
Inputs may be any that keep to these rules, and one draw needn't show every extreme that they name: `neighbours`: for frame block b and tile t, the entries that are not -1 are distinct frame blocks from max(0, b - 5) to b - 1; lists hold 0 to 3 entries, and some list is full. `halo_rows`: some frame block and tile reads 2 rows.
All inputs are finite; a program needn't handle non-finite values.
Results may differ from a plain program's by a relative error of at most 0.0046.
Values may be sent and summed in bfloat16 or wider, within the bound.
A program may use at most 128 MiB of HBM per device.

v0:
```python
import functools
import math

import jax
import jax.numpy as jnp
from jax import lax
from jax.experimental import pallas as pl
from jax.experimental.pallas import tpu as pltpu
from jax.sharding import PartitionSpec as P

HD = 128
HMAX = 2
WIN = 5
UP, DOWN = WIN + 1, WIN + 2
SLOTS = WIN + 3
AHEAD = 2
LOW = -1e30
SCALE = math.log2(math.e) / math.sqrt(HD)

ROUTES = (
    ((0, 0, 4, None), (0, 0, 2, None), (0, 0, 1, None), (1, 4, 5, None), (1, 2, 3, None)),
    (
        (0, 0, 2, None),
        (0, 0, 4, 0),
        (1, 2, 5, 1),
        (1, 4, 5, 0),
        (1, 2, 1, None),
        (1, 4, 3, 0),
        (2, 5, 3, 1),
        (3, 3, 4, 1),
    ),
    ((0, 0, 4, None), (0, 0, 1, None), (1, 4, 2, None), (1, 4, 5, None), (2, 2, 3, None)),
    ((0, 0, 4, None), (1, 4, 2, None), (1, 4, 3, None), (2, 2, 5, None), (2, 2, 1, None)),
)
GROUP = len(ROUTES)
STAGES = 4


def sends_of(role):
    found = []
    for origin, rows in enumerate(ROUTES):
        for stage, src, dst, parity in rows:
            if (origin + src) % GROUP == role:
                found.append((stage, src, dst - src, dst, parity))
    return found


MOST = max(len(sends_of(role)) for role in range(GROUP))


def both(*terms):
    out = terms[0]
    for term in terms[1:]:
        out = jnp.logical_and(out, term)
    return out


def kernel(count, tiles, shape, lists_ref, halo_ref, q_ref, k_ref, v_ref, out_ref,
           kv, q_v, bias, local_sem, q_sem, send_sem, recv_sem):
    frames, rows, columns = shape
    tokens = frames * rows * columns
    heads = q_ref.shape[1] // HD
    block = lax.axis_index("tm")
    tile = lax.axis_index("tile")
    role = block % GROUP

    def part(ref, head):
        return ref.at[:, pl.ds(pl.multiple_of(head * HD, HD), HD)]

    def fetch(head, carry):
        pltpu.make_async_copy(part(k_ref, head), kv.at[0, head, 0], local_sem.at[head]).start()
        pltpu.make_async_copy(part(v_ref, head), kv.at[0, head, 1], local_sem.at[head]).start()
        return carry

    lax.fori_loop(0, heads, fetch, 0)
    q_copy = pltpu.make_async_copy(q_ref, q_v, q_sem)
    q_copy.start()

    barrier = pltpu.get_barrier_semaphore()
    expected = jnp.int32(0)
    partners = [("tm", block, count, step) for step in range(-WIN, WIN + 1) if step]
    partners += [("tile", tile, tiles, step) for step in (-1, 1)]
    for axis, me, size, step in partners:
        there = both(me + step >= 0, me + step < size)

        @pl.when(there)
        def _():
            pl.semaphore_signal(barrier, inc=1, device_id={axis: me + step},
                                device_id_type=pl.DeviceIdType.MESH)

        expected += there.astype(jnp.int32)

    missing = [(d, block < d) for d in range(1, WIN + 1)]
    missing += [(UP, tile < 1), (DOWN, tile + 1 >= tiles)]
    for slot, gone in missing:

        @pl.when(gone)
        def _():
            def clear(head, carry):
                kv[slot, head] = jnp.zeros(kv.shape[2:], kv.dtype)
                return carry

            lax.fori_loop(0, heads, clear, 0)

    reach = halo_ref[0]
    query = lax.broadcasted_iota(jnp.int32, (tokens, tokens), 0) // (rows * columns)
    key = lax.broadcasted_iota(jnp.int32, (tokens, tokens), 1)
    key_row = (key // columns) % rows
    causal = key // (rows * columns) <= query
    above = both(causal, key_row >= rows - reach, tile >= 1)
    below = both(causal, key_row < reach, tile + 1 < tiles)
    for at, mask in enumerate((causal, above, below)):
        bias[at] = jnp.where(mask, 0.0, LOW)

    present = []
    for d in range(1, WIN + 1):
        hit = lists_ref[0] == block - d
        for n in range(1, lists_ref.shape[0]):
            hit = jnp.logical_or(hit, lists_ref[n] == block - d)
        present.append(jnp.logical_and(hit, block >= d))

    pl.semaphore_wait(barrier, expected)

    def remote(src, dst, head, sem, target):
        return pltpu.make_async_remote_copy(
            src_ref=kv.at[src, head],
            dst_ref=kv.at[dst, head],
            send_sem=send_sem.at[sem],
            recv_sem=recv_sem.at[dst, head],
            device_id=target,
            device_id_type=pl.DeviceIdType.MESH,
        )

    def arrived(slot, head):
        remote(slot, slot, head, 0, {"tm": block}).wait_recv()

    def own(head):
        pltpu.make_async_copy(kv.at[0, head], kv.at[0, head], local_sem.at[head]).wait()

        @pl.when(tile + 1 < tiles)
        def _():
            remote(0, UP, head, MOST, {"tile": tile + 1}).start()

        @pl.when(tile >= 1)
        def _():
            remote(0, DOWN, head, MOST + 1, {"tile": tile - 1}).start()

        relay(0, head)

    def relay(stage, head):
        for mine in range(GROUP):
            entries = [(at, *e) for at, e in enumerate(sends_of(mine)) if e[0] == stage]
            if not entries:
                continue

            @pl.when(role == mine)
            def _():
                for slot in sorted({e[2] for e in entries}):
                    group = [e for e in entries if e[2] == slot]
                    parities = {e[5] for e in group}
                    if slot:
                        needed = block >= slot
                        if None not in parities:
                            needed = both(needed, head % 2 == min(parities))

                        @pl.when(needed)
                        def _():
                            arrived(slot, head)

                    for at, _, _, step, dst, parity in group:
                        go = both(block >= slot, block + step < count)
                        if parity is not None:
                            go = both(go, head % 2 == parity)

                        @pl.when(go)
                        def _():
                            remote(slot, dst, head, at, {"tm": block + step}).start()

    def leaves(head):
        for mine in range(GROUP):
            entries = sends_of(mine)

            @pl.when(role == mine)
            def _():
                for slot in range(1, WIN + 1):
                    parities = {e[4] for e in entries if e[1] == slot}
                    if None in parities or parities == {0, 1}:
                        continue
                    needed = block >= slot
                    if parities:
                        needed = both(needed, head % 2 != min(parities))

                    @pl.when(needed)
                    def _():
                        arrived(slot, head)

        @pl.when(tile >= 1)
        def _():
            arrived(UP, head)

        @pl.when(tile + 1 < tiles)
        def _():
            arrived(DOWN, head)

    def attend(head):
        query_part = part(q_v, head)[...]
        scores = []
        tops = []
        for slot in range(SLOTS):
            s = lax.dot_general(query_part, kv[slot, head, 0], (((1,), (1,)), ((), ())),
                                preferred_element_type=jnp.float32)
            if slot == 0:
                s = s + bias[0]
            elif slot > WIN:
                s = s + bias[slot - WIN]
            top = jnp.max(s, axis=1, keepdims=True)
            if 0 < slot <= WIN:
                top = jnp.where(present[slot - 1], top, LOW)
            scores.append(s)
            tops.append(top)
        top = functools.reduce(jnp.maximum, tops) * SCALE
        total = None
        numerator = None
        for slot in range(SLOTS):
            shift = jnp.where(present[slot - 1], top, -LOW) if 0 < slot <= WIN else top
            w = jnp.exp2(scores[slot] * SCALE - shift)
            total = w if total is None else total + w
            term = jnp.dot(w.astype(jnp.bfloat16), kv[slot, head, 1],
                           preferred_element_type=jnp.float32)
            numerator = term if numerator is None else numerator + term
        total = jnp.sum(total, axis=1, keepdims=True)
        part(out_ref, head)[...] = (numerator / total).astype(out_ref.dtype)

    def first(head, carry):
        own(head)
        return carry

    lax.fori_loop(0, AHEAD, first, 0)
    q_copy.wait()

    def step(t, carry):
        @pl.when(t + AHEAD < heads)
        def _():
            own(t + AHEAD)

        for stage in range(1, STAGES):
            head = t - (stage - 1)

            @pl.when(both(head >= 0, head < heads))
            def _():
                relay(stage, head)

        head = t - (STAGES - 1)

        @pl.when(head >= 0)
        def _():
            leaves(head)
            attend(head)

        return carry

    lax.fori_loop(0, heads + STAGES - 1, step, 0)

    def sent(slot, parity, sem):
        size = heads if parity is None else (heads + 1 - parity) // 2
        ref = kv.at[slot, pl.ds(0, size)]
        pltpu.make_async_remote_copy(
            src_ref=ref, dst_ref=ref, send_sem=send_sem.at[sem], recv_sem=recv_sem.at[0, 0],
            device_id={"tm": block}, device_id_type=pl.DeviceIdType.MESH,
        ).wait_send()

    for mine in range(GROUP):

        @pl.when(role == mine)
        def _():
            for at, (_, slot, step_, dst, parity) in enumerate(sends_of(mine)):

                @pl.when(both(block >= slot, block + step_ < count))
                def _():
                    sent(slot, parity, at)

    @pl.when(tile + 1 < tiles)
    def _():
        sent(0, None, MOST)

    @pl.when(tile >= 1)
    def _():
        sent(0, None, MOST + 1)


def local(count, tiles, queries, keys, values, neighbours, halo_rows):
    frames, rows, columns, channels = queries.shape
    tokens = frames * rows * columns
    heads = channels // HD
    assert rows == HMAX and count % GROUP == 0
    flat = (tokens, channels)
    smem = pl.BlockSpec(memory_space=pltpu.SMEM)
    anywhere = pl.BlockSpec(memory_space=pl.ANY)
    out = pl.pallas_call(
        functools.partial(kernel, count, tiles, (frames, rows, columns)),
        out_shape=jax.ShapeDtypeStruct(flat, jnp.bfloat16),
        in_specs=[smem, smem, anywhere, anywhere, anywhere],
        out_specs=pl.BlockSpec(memory_space=pltpu.VMEM),
        scratch_shapes=[
            pltpu.VMEM((SLOTS, heads, 2, tokens, HD), jnp.bfloat16),
            pltpu.VMEM(flat, jnp.bfloat16),
            pltpu.VMEM((3, tokens, tokens), jnp.float32),
            pltpu.SemaphoreType.DMA((heads,)),
            pltpu.SemaphoreType.DMA,
            pltpu.SemaphoreType.DMA((MOST + 2,)),
            pltpu.SemaphoreType.DMA((SLOTS, heads)),
        ],
        compiler_params=pltpu.CompilerParams(
            collective_id=0, has_side_effects=True, vmem_limit_bytes=56 * 1024 * 1024
        ),
    )(
        neighbours.reshape(-1),
        halo_rows.reshape(-1),
        queries.reshape(flat),
        keys.reshape(flat),
        values.reshape(flat),
    )
    return out.reshape(queries.shape)


def solution(mesh):
    return jax.shard_map(
        functools.partial(local, mesh.shape["tm"], mesh.shape["tile"]),
        mesh=mesh,
        in_specs=(
            P("tm", "tile", None, None),
            P("tm", "tile", None, None),
            P("tm", "tile", None, None),
            P("tm", "tile", None),
            P("tm", "tile"),
        ),
        out_specs=P("tm", "tile", None, None),
        check_vma=False,
    )
```

profile of v0, /device:TPU:17, one launch (start us, length us, event | category | flops | bytes accessed | tf_op | source)
XLA Modules:
  0.0 96.3 jit_solution(147547011229466658)
XLA Ops:
  0.7 93.2 %shard_map.55 = bf16[256,2560]{1,0:T(8,128)(2,1)} custom-call(s32[3]{0:T(128)} %bitcast.11, s32[1]{0:T(128)} %bitcast.6.halo_ref, bf16[256,2560]{1,0:T(8,128)(2,1)} %bitcast.8, bf16[256,2560]{1,0:T(8,128)(2,1)} %bitcast.9, bf16[256,2560]{1,0:T(8,128)(2,1)} %bitcast.10), custom_call_target="tpu_custom_call" | custom-call | tf_op jit(solution)/shard_map/pallas_call | solution.py:299
  93.8 2.5 %copy.8 = bf16[2,2,64,2560]{3,2,1,0:T(8,128)(2,1)} copy(bf16[2,2,64,2560]{3,2,1,0:T(8,128)(2,1)} %bitcast.7) | data formatting | bytes 2621440
where the time goes:
time: 97.9 us; the launch traced here: 96.3 us
  Pallas kernels  93.2 us (95%)
  local copies, waits for them, and re-layouts  2.46 us (3%)
    pallas_call x1, Pallas kernels, local(): pl.pallas_call(functools.partial(kernel, count, tiles, (frames, rows, col...  93.2 us
    unnamed x1, local copies, waits for them, and re-layouts  2.46 us

commit v1 on v0

v1 whole, which is shorter than its diff:
```python
import functools
import math

import jax
import jax.numpy as jnp
from jax import lax
from jax.experimental import pallas as pl
from jax.experimental.pallas import tpu as pltpu
from jax.sharding import PartitionSpec as P

HD = 128
HMAX = 2
WIN = 5
GROUP = 4
ASKS = 2
FIRST = ASKS - 1
PAST = GROUP - FIRST
ROWS = 8
LOW = -1e30
SCALE = math.log2(math.e) / math.sqrt(HD)


def both(*terms):
    out = terms[0]
    for term in terms[1:]:
        out = jnp.logical_and(out, term)
    return out


def kernel(count, tiles, shape, lists_ref, halo_ref, q_ref, k_ref, v_ref, out_ref,
           own, side, past, ask, part, stat, back, back_stat, res, info, far, bias,
           local_sem, in_sem, in_send, side_sem, side_send, past_sem, past_send,
           ask_sem, ask_send, back_sem, back_send, stat_sem, stat_send,
           out_sem, out_send, info_sem, info_send, asked_sem, asked_send):
    frames, rows, columns = shape
    tokens = frames * rows * columns
    share = own.shape[1]
    slots = lists_ref.shape[0]
    block = lax.axis_index("tm")
    tile = lax.axis_index("tile")
    me = block % GROUP
    base = block - me
    partner = me + 1 - 2 * (me % 2)
    across = (me + 2) % GROUP
    beyond = (partner + 2) % GROUP
    behind = block >= GROUP
    ahead = block + GROUP < count

    def columns_of(head):
        return pl.ds(pl.multiple_of(head * HD, HD), HD)

    def remote(src, dst, send, recv, target):
        return pltpu.make_async_remote_copy(
            src_ref=src, dst_ref=dst, send_sem=send, recv_sem=recv,
            device_id=target, device_id_type=pl.DeviceIdType.MESH,
        )

    def landed(ref, sem):
        remote(ref, ref, in_send.at[0], sem, {"tm": block}).wait_recv()

    def sent(ref, sem):
        remote(ref, ref, sem, out_sem, {"tm": block}).wait_send()

    if tiles == 2:
        sides = [(tile >= 1, 1 - 2 * tile, None)]
    elif tiles > 2:
        sides = [(None, -1, tile >= 1), (None, 1, tile + 1 < tiles)]
    else:
        sides = []

    def maybe(condition, action):
        if condition is None:
            action()
        else:
            pl.when(condition)(action)

    def fetch(h, carry):
        for i, ref in enumerate((q_ref, k_ref, v_ref)):
            pltpu.make_async_copy(ref.at[:, columns_of(me * share + h)],
                                  own.at[me, h, i], local_sem.at[h]).start()
        return carry

    lax.fori_loop(0, share, fetch, 0)

    barrier = pltpu.get_barrier_semaphore()
    expected = jnp.int32(GROUP - 1)

    def greet(target):
        pl.semaphore_signal(barrier, inc=1, device_id=target, device_id_type=pl.DeviceIdType.MESH)

    for role in (partner, across, beyond):
        greet({"tm": base + role})
    for there, step in ((behind, -GROUP), (ahead, GROUP)):
        pl.when(there)(lambda: greet({"tm": block + step}))
        expected += there.astype(jnp.int32)
    for _, step, there in sides:
        maybe(there, lambda: greet({"tile": tile + step}))
        expected += 1 if there is None else there.astype(jnp.int32)

    row = lax.broadcasted_iota(jnp.int32, (ROWS, tokens), 0)
    mine = jnp.where(row == slots, halo_ref[0], -1)
    for n in range(slots):
        mine = jnp.where(row == n, lists_ref[n], mine)
    info[me] = mine

    pl.semaphore_wait(barrier, expected)

    for role in (partner, across, beyond):
        remote(info.at[me], info.at[me], info_send, info_sem.at[me], {"tm": base + role}).start()

    def give(role, at, h):
        for i, ref in ((1, k_ref), (2, v_ref), (0, q_ref)):
            remote(ref.at[:, columns_of(role * share + h)], own.at[me, h, i],
                   in_send.at[at], in_sem.at[me, h], {"tm": base + role}).start()

    def give_partner(h, carry):
        give(partner, 0, h)
        return carry

    def give_across(h):
        give(across, 1, h)
        give(beyond, 2, h)

    give_across(0)
    lax.fori_loop(0, share, give_partner, 0)
    give_across(1)

    def forward(role, h):
        pair = pl.ds(1, 2)
        for at, (_, step, there) in enumerate(sides):
            other = len(sides) - 1 - at
            maybe(there, lambda: remote(
                own.at[role, h, pair], side.at[other, role, h], side_send.at[at],
                side_sem.at[other, role, h], {"tile": tile + step}).start())

        @pl.when(both(role >= FIRST, ahead))
        def _():
            remote(own.at[role, h, pair], past.at[role - FIRST, h], past_send,
                   past_sem.at[role - FIRST, h], {"tm": block + GROUP}).start()

        @pl.when(both(role < ASKS, behind))
        def _():
            remote(own.at[role, h, 0], ask.at[role, h], ask_send,
                   ask_sem.at[role, h], {"tm": block - GROUP}).start()

    def forward_near(h):
        pltpu.make_async_copy(own.at[me, h], own.at[me, h], local_sem.at[h]).wait()
        forward(me, h)
        landed(own.at[partner, h], in_sem.at[partner, h])
        forward(partner, h)

    def forward_far(h):
        for role in (across, beyond):
            landed(own.at[role, h], in_sem.at[role, h])
            forward(role, h)

    forward_near(0)
    forward_near(1)

    @pl.when(jnp.logical_not(behind))
    def _():
        past[...] = jnp.zeros(past.shape, past.dtype)
        back[...] = jnp.zeros(back.shape, back.dtype)
        back_stat[...] = jnp.full(back_stat.shape, LOW, back_stat.dtype)

    for at, (_, _, there) in enumerate(sides):
        if there is not None:

            @pl.when(jnp.logical_not(there))
            def _():
                side[at] = jnp.zeros(side.shape[1:], side.dtype)

    for role in (partner, across, beyond):
        landed(info.at[role], info_sem.at[role])

    @pl.when(behind)
    def _():
        remote(info.at[pl.ds(0, ASKS)], info.at[pl.ds(GROUP, ASKS)], asked_send, asked_sem,
               {"tm": block - GROUP}).start()

    def spread(at, number):
        out = jnp.full((ROWS, tokens), LOW, jnp.float32)
        for d in range(1, WIN + 1):
            wanted = jnp.where(number >= d, number - d, -2)
            hit = info[at, 0:1, :] == wanted
            for n in range(1, slots):
                hit = jnp.logical_or(hit, info[at, n : n + 1, :] == wanted)
            out = jnp.where(jnp.logical_and(row == d, hit), 0.0, out)
        far[at] = out

    query = lax.broadcasted_iota(jnp.int32, (tokens, tokens), 0) // (rows * columns)
    key = lax.broadcasted_iota(jnp.int32, (tokens, tokens), 1)
    causal = key // (rows * columns) <= query
    bias[0] = jnp.where(causal, 0.0, LOW)
    key_row = (lax.broadcasted_iota(jnp.int32, (1, tokens), 1) // columns) % rows
    for role in range(GROUP):
        spread(role, base + role)
        reach = info[role, slots : slots + 1, :]
        above = jnp.where(key_row >= rows - reach, 0.0, LOW)
        below = jnp.where(key_row < reach, 0.0, LOW)
        for at, (upper, step, there) in enumerate(sides):
            if upper is not None:
                edge = jnp.where(upper, above, below)
            else:
                edge = jnp.where(there, above if step < 0 else below, LOW)
            bias[1 + role * len(sides) + at] = jnp.where(causal, edge, LOW)

    @pl.when(ahead)
    def _():
        landed(info.at[pl.ds(GROUP, ASKS)], asked_sem)
        for role in range(ASKS):
            spread(GROUP + role, base + GROUP + role)

    def attend(query_part, parts):
        scores = []
        most = None
        for k_part, _, shift in parts:
            s = lax.dot_general(query_part, k_part[...], (((1,), (1,)), ((), ())),
                                preferred_element_type=jnp.float32) + shift
            most = s if most is None else jnp.maximum(most, s)
            scores.append(s)
        top = jnp.max(most, axis=1, keepdims=True) * SCALE
        total = None
        numerator = None
        for s, (_, v_part, _) in zip(scores, parts):
            w = jnp.exp2(s * SCALE - top)
            total = w if total is None else total + w
            term = jnp.dot(w.astype(jnp.bfloat16), v_part[...], preferred_element_type=jnp.float32)
            numerator = term if numerator is None else numerator + term
        return numerator, jnp.sum(total, axis=1, keepdims=True), top

    def distant(at, d):
        return far[at, d : d + 1, :]

    def visit(h):
        for role in range(ASKS):
            landed(ask.at[role, h], ask_sem.at[role, h])
            parts = []
            for other in range(GROUP):
                d = role + GROUP - other
                if d <= WIN:
                    parts.append((own.at[other, h, 1], own.at[other, h, 2], distant(GROUP + role, d)))
            for other in range(GROUP - 1, GROUP):
                d = role + 2 * GROUP - other
                if d <= WIN:
                    kv = past.at[other - FIRST, h]
                    parts.append((kv.at[0], kv.at[1], distant(GROUP + role, d)))
            numerator, total, top = attend(ask[role, h], parts)
            part[role, h] = (numerator / total).astype(part.dtype)
            level = jnp.broadcast_to(top + jnp.log2(total), (tokens, HD))
            stat[role, h] = jnp.transpose(level)[0:1, :]
        for role in range(ASKS):
            remote(part.at[role, h], back.at[role, h], back_send, back_sem.at[role, h],
                   {"tm": block + GROUP}).start()
            remote(stat.at[role, h], back_stat.at[role, h], stat_send, stat_sem.at[role, h],
                   {"tm": block + GROUP}).start()

    def unit(role, h):
        for at, (_, _, there) in enumerate(sides):
            maybe(there, lambda: landed(side.at[at, role, h], side_sem.at[at, role, h]))
        if role < ASKS:

            @pl.when(behind)
            def _():
                landed(back.at[role, h], back_sem.at[role, h])
                landed(back_stat.at[role, h], stat_sem.at[role, h])

        parts = [(own.at[role, h, 1], own.at[role, h, 2], bias[0])]
        for other in range(role):
            parts.append((own.at[other, h, 1], own.at[other, h, 2], distant(role, role - other)))
        if role >= ASKS:
            for other in range(FIRST, GROUP):
                d = role + GROUP - other
                if d <= WIN:
                    kv = past.at[other - FIRST, h]
                    parts.append((kv.at[0], kv.at[1], distant(role, d)))
        for at in range(len(sides)):
            kv = side.at[at, role, h]
            parts.append((kv.at[0], kv.at[1], bias[1 + role * len(sides) + at]))
        numerator, total, top = attend(own[role, h, 0], parts)
        if role < ASKS:
            level = jnp.transpose(jnp.broadcast_to(back_stat[role, h], (HD, tokens)))
            peak = jnp.maximum(level, top)
            here = jnp.exp2(top - peak)
            there = jnp.exp2(level - peak)
            numerator = numerator * here + back[role, h].astype(jnp.float32) * there
            total = total * here + there
        res[role, h] = (numerator / total).astype(res.dtype)

    def deliver(role, h):
        place = columns_of(me * share + h)

        @pl.when(me == role)
        def _():
            out_ref[:, place] = res[role, h]

        @pl.when(me != role)
        def _():
            remote(res.at[role, h], out_ref.at[:, place], out_send, out_sem,
                   {"tm": base + role}).start()

    def answer(h):
        @pl.when(behind)
        def _():
            for at in range(PAST - 1):
                landed(past.at[at, h], past_sem.at[at, h])

        def half(phase, carry):
            pair = (me // 2 + 1 + phase) % 2
            for mine_ in range(2):

                @pl.when(pair == mine_)
                def _():
                    for role in (2 * mine_, 2 * mine_ + 1):
                        unit(role, h)
                    for role in (2 * mine_, 2 * mine_ + 1):
                        deliver(role, h)

            return carry

        lax.fori_loop(0, 2, half, 0)

    def step(t, carry):
        @pl.when(t + 2 < share)
        def _():
            give_across(t + 2)

        @pl.when(t < share)
        def _():
            forward_far(t)

        @pl.when(both(t % 2 == 0, 2 + t // 2 < share))
        def _():
            forward_near(2 + t // 2)

        @pl.when(both(t >= 1, t - 1 < share, behind))
        def _():
            landed(past.at[PAST - 1, t - 1], past_sem.at[PAST - 1, t - 1])

        @pl.when(both(t >= 1, t - 1 < share, ahead))
        def _():
            visit(t - 1)

        @pl.when(t >= 2)
        def _():
            answer(t - 2)

        return carry

    assert share >= 2 and 2 + (share + 1) // 2 >= share
    lax.fori_loop(0, share + 2, step, 0)

    landed(res.at[pl.ds(0, GROUP - 1)], out_sem)
    sent(res.at[pl.ds(0, GROUP - 1)], out_send)
    sent(info.at[pl.ds(0, GROUP - 1)], info_send)
    for at in range(GROUP - 1):
        sent(own.at[0], in_send.at[at])
    for at, (_, _, there) in enumerate(sides):
        maybe(there, lambda: sent(side.at[at], side_send.at[at]))

    @pl.when(ahead)
    def _():
        sent(past, past_send)
        sent(back, back_send)
        sent(back_stat, stat_send)

    @pl.when(behind)
    def _():
        sent(ask, ask_send)
        sent(info.at[pl.ds(0, ASKS)], asked_send)


def local(count, tiles, queries, keys, values, neighbours, halo_rows):
    frames, rows, columns, channels = queries.shape
    tokens = frames * rows * columns
    heads = channels // HD
    share = heads // GROUP
    assert rows == HMAX and count % GROUP == 0 and heads % GROUP == 0
    sides = min(2, tiles - 1)
    flat = (tokens, channels)
    piece = (tokens, HD)
    smem = pl.BlockSpec(memory_space=pltpu.SMEM)
    anywhere = pl.BlockSpec(memory_space=pl.ANY)
    dma = pltpu.SemaphoreType.DMA

    def vmem(*size, dtype=jnp.bfloat16):
        return pltpu.VMEM(size, dtype)

    out = pl.pallas_call(
        functools.partial(kernel, count, tiles, (frames, rows, columns)),
        out_shape=jax.ShapeDtypeStruct(flat, jnp.bfloat16),
        in_specs=[smem, smem, anywhere, anywhere, anywhere],
        out_specs=pl.BlockSpec(memory_space=pltpu.VMEM),
        scratch_shapes=[
            vmem(GROUP, share, 3, *piece),
            vmem(max(1, sides), GROUP, share, 2, *piece),
            vmem(PAST, share, 2, *piece),
            vmem(ASKS, share, *piece),
            vmem(ASKS, share, *piece),
            vmem(ASKS, share, 1, tokens, dtype=jnp.float32),
            vmem(ASKS, share, *piece),
            vmem(ASKS, share, 1, tokens, dtype=jnp.float32),
            vmem(GROUP, share, *piece),
            vmem(GROUP + ASKS, ROWS, tokens, dtype=jnp.int32),
            vmem(GROUP + ASKS, ROWS, tokens, dtype=jnp.float32),
            vmem(1 + GROUP * sides, tokens, tokens, dtype=jnp.float32),
            dma((share,)),
            dma((GROUP, share)),
            dma((GROUP - 1,)),
            dma((max(1, sides), GROUP, share)),
            dma((max(1, sides),)),
            dma((PAST, share)),
            dma,
            dma((ASKS, share)),
            dma,
            dma((ASKS, share)),
            dma,
            dma((ASKS, share)),
            dma,
            dma,
            dma,
            dma((GROUP,)),
            dma,
            dma,
            dma,
        ],
        compiler_params=pltpu.CompilerParams(
            collective_id=0, has_side_effects=True, vmem_limit_bytes=56 * 1024 * 1024
        ),
    )(
        neighbours.reshape(-1),
        halo_rows.reshape(-1),
        queries.reshape(flat),
        keys.reshape(flat),
        values.reshape(flat),
    )
    return out.reshape(queries.shape)


def solution(mesh):
    return jax.shard_map(
        functools.partial(local, mesh.shape["tm"], mesh.shape["tile"]),
        mesh=mesh,
        in_specs=(
            P("tm", "tile", None, None),
            P("tm", "tile", None, None),
            P("tm", "tile", None, None),
            P("tm", "tile", None),
            P("tm", "tile"),
        ),
        out_specs=P("tm", "tile", None, None),
        check_vma=False,
    )
```

time: 97.9 us -> 73 us (0.75)
  Pallas kernels: 93.2 us -> 69.1 us
    pallas_call x1, Pallas kernels: 93.2 us -> 69.1 us  [local(): pl.pallas_call(functools.partial(kernel, count, tiles, (frames, rows, col...]
where the time goes in v1:
time: 73 us; the launch traced here: 72.2 us
  Pallas kernels  69.1 us (95%)
  local copies, waits for them, and re-layouts  2.46 us (3%)
    pallas_call x1, Pallas kernels, local(): pl.pallas_call(functools.partial(kernel, count, tiles, (frames, rows, col...  69.1 us
    unnamed x1, local copies, waits for them, and re-layouts  2.46 us

profile of v1, /device:TPU:17, one launch (start us, length us, event | category | flops | bytes accessed | tf_op | source)
XLA Modules:
  0.0 72.2 jit_solution(7551472065212005399)
XLA Ops:
  0.7 69.1 %shard_map.55 = bf16[256,2560]{1,0:T(8,128)(2,1)} custom-call(s32[3]{0:T(128)} %bitcast.11, s32[1]{0:T(128)} %bitcast.6.halo_ref, bf16[256,2560]{1,0:T(8,128)(2,1)} %bitcast.8, bf16[256,2560]{1,0:T(8,128)(2,1)} %bitcast.9, bf16[256,2560]{1,0:T(8,128)(2,1)} %bitcast.10), custom_call_target="tpu_custom_call" | custom-call | tf_op jit(solution)/shard_map/pallas_call | solution.py:389
  69.7 2.5 %copy.8 = bf16[2,2,64,2560]{3,2,1,0:T(8,128)(2,1)} copy(bf16[2,2,64,2560]{3,2,1,0:T(8,128)(2,1)} %bitcast.7) | data formatting | bytes 2621440

commit v2 on v1

v2 whole, which is shorter than its diff:
```python
import functools
import math

import jax
import jax.numpy as jnp
from jax import lax
from jax.experimental import pallas as pl
from jax.experimental.pallas import tpu as pltpu
from jax.sharding import PartitionSpec as P

HD = 128
HMAX = 2
WIN = 5
GROUP = 4
ROWS = 8
LOW = -1e30
SCALE = math.log2(math.e) / math.sqrt(HD)


def both(*terms):
    out = terms[0]
    for term in terms[1:]:
        out = jnp.logical_and(out, term)
    return out


def kernel(count, tiles, shape, lists_ref, halo_ref, q_ref, k_ref, v_ref, out_ref,
           qs, kv, side, past, ask, part, stat, back, back_stat, res, info, far, bias,
           local_sem, q_sem, kv_sem, in_send, side_sem, side_send, past_sem, past_send,
           ask_sem, ask_send, back_sem, back_send, stat_sem, stat_send,
           out_sem, out_send, info_sem, info_send, asked_sem, asked_send):
    frames, rows, columns = shape
    tokens = frames * rows * columns
    share = kv.shape[1]
    slots = lists_ref.shape[0]
    block = lax.axis_index("tm")
    tile = lax.axis_index("tile")
    me = block % GROUP
    base = block - me
    partner = me + 1 - 2 * (me % 2)
    across = (me + 2) % GROUP
    beyond = (partner + 2) % GROUP
    behind = block >= GROUP
    ahead = block + GROUP < count
    last = GROUP - 1

    def columns_of(head):
        return pl.ds(pl.multiple_of(head * HD, HD), HD)

    def remote(src, dst, send, recv, target):
        return pltpu.make_async_remote_copy(
            src_ref=src, dst_ref=dst, send_sem=send, recv_sem=recv,
            device_id=target, device_id_type=pl.DeviceIdType.MESH,
        )

    def landed(ref, sem):
        remote(ref, ref, in_send.at[0], sem, {"tm": block}).wait_recv()

    def sent(ref, sem):
        remote(ref, ref, sem, out_sem, {"tm": block}).wait_send()

    if tiles == 2:
        sides = [(tile >= 1, 1 - 2 * tile, None)]
    elif tiles > 2:
        sides = [(None, -1, tile >= 1), (None, 1, tile + 1 < tiles)]
    else:
        sides = []

    def maybe(condition, action):
        if condition is None:
            action()
        else:
            pl.when(condition)(action)

    barrier = pltpu.get_barrier_semaphore()
    expected = jnp.int32(GROUP - 1)

    def greet(target):
        pl.semaphore_signal(barrier, inc=1, device_id=target, device_id_type=pl.DeviceIdType.MESH)

    for role in (across, beyond, partner):
        greet({"tm": base + role})
    for _, step, there in sides:
        maybe(there, lambda: greet({"tile": tile + step}))
        expected += 1 if there is None else there.astype(jnp.int32)
    for there, step in ((behind, -GROUP), (ahead, GROUP)):
        pl.when(there)(lambda: greet({"tm": block + step}))
        expected += there.astype(jnp.int32)

    def spots(role, h):
        return ((k_ref, kv.at[role, h, 0]), (v_ref, kv.at[role, h, 1]), (q_ref, qs.at[role, h]))

    def fetch(h, carry):
        for ref, spot in spots(me, h):
            pltpu.make_async_copy(ref.at[:, columns_of(me * share + h)], spot, local_sem.at[h]).start()
        return carry

    lax.fori_loop(0, share, fetch, 0)

    row = lax.broadcasted_iota(jnp.int32, (ROWS, tokens), 0)
    mine = jnp.where(row == slots, halo_ref[0], -1)
    for n in range(slots):
        mine = jnp.where(row == n, lists_ref[n], mine)
    info[me] = mine

    pl.semaphore_wait(barrier, expected)

    def give(role, at, h, which):
        for ref, spot in which(spots(me, h)):
            sem = q_sem if ref is q_ref else kv_sem
            remote(ref.at[:, columns_of(role * share + h)], spot, in_send.at[at], sem.at[me, h],
                   {"tm": base + role}).start()

    def keys_of(pairs):
        return pairs[:2]

    def queries_of(pairs):
        return pairs[2:]

    def give_across(h, which):
        give(across, 1, h, which)
        give(beyond, 2, h, which)

    def give_partner(h, carry):
        give(partner, 0, h, keys_of)
        give(partner, 0, h, queries_of)
        return carry

    def to_sides(role, h):
        for at, (_, step, there) in enumerate(sides):
            other = len(sides) - 1 - at
            maybe(there, lambda: remote(
                kv.at[role, h], side.at[other, role, h], side_send.at[at],
                side_sem.at[other, role, h], {"tile": tile + step}).start())

    def to_next(role, h):
        @pl.when(both(role == last, ahead))
        def _():
            remote(kv.at[role, h], past.at[h], past_send, past_sem.at[h],
                   {"tm": block + GROUP}).start()

    def to_before(role, h):
        @pl.when(behind)
        def _():
            remote(qs.at[role, h], ask.at[role, h], ask_send, ask_sem.at[role, h],
                   {"tm": block - GROUP}).start()

    def own_here(h):
        for _, spot in spots(me, h):
            pltpu.make_async_copy(spot, spot, local_sem.at[h]).wait()

    def partner_here(h):
        landed(kv.at[partner, h], kv_sem.at[partner, h])
        landed(qs.at[partner, h], q_sem.at[partner, h])

    def near_z(role, h):
        to_before(role, h)
        to_next(role, h)

    for role in (partner, across, beyond):
        remote(info.at[me], info.at[me], info_send, info_sem.at[me], {"tm": base + role}).start()
    give_across(0, keys_of)
    own_here(0)
    to_sides(me, 0)
    give_across(0, queries_of)
    give_across(1, queries_of)
    lax.fori_loop(0, share, give_partner, 0)
    if share > 2:
        give_across(2, queries_of)
    give_across(1, keys_of)
    near_z(me, 0)
    partner_here(0)
    to_sides(partner, 0)
    near_z(partner, 0)

    for role in (partner, across, beyond):
        landed(info.at[role], info_sem.at[role])

    @pl.when(behind)
    def _():
        remote(info.at[pl.ds(0, GROUP)], info.at[pl.ds(GROUP, GROUP)], asked_send, asked_sem,
               {"tm": block - GROUP}).start()

    def settle(h):
        own_here(h)
        near_z(me, h)
        partner_here(h)
        near_z(partner, h)

    def near_sides(h):
        to_sides(partner, h)
        to_sides(me, h)

    settle(1)
    near_sides(1)

    @pl.when(jnp.logical_not(behind))
    def _():
        past[...] = jnp.zeros(past.shape, past.dtype)
        back[...] = jnp.zeros(back.shape, back.dtype)
        back_stat[...] = jnp.full(back_stat.shape, LOW, back_stat.dtype)

    for at, (_, _, there) in enumerate(sides):
        if there is not None:

            @pl.when(jnp.logical_not(there))
            def _():
                side[at] = jnp.zeros(side.shape[1:], side.dtype)

    def spread(at, number):
        out = jnp.full((ROWS, tokens), LOW, jnp.float32)
        for d in range(1, WIN + 1):
            wanted = jnp.where(number >= d, number - d, -2)
            hit = info[at, 0:1, :] == wanted
            for n in range(1, slots):
                hit = jnp.logical_or(hit, info[at, n : n + 1, :] == wanted)
            out = jnp.where(jnp.logical_and(row == d, hit), 0.0, out)
        far[at] = out

    query = lax.broadcasted_iota(jnp.int32, (tokens, tokens), 0) // (rows * columns)
    key = lax.broadcasted_iota(jnp.int32, (tokens, tokens), 1)
    causal = key // (rows * columns) <= query
    bias[0] = jnp.where(causal, 0.0, LOW)
    key_row = (lax.broadcasted_iota(jnp.int32, (1, tokens), 1) // columns) % rows
    for role in range(GROUP):
        spread(role, base + role)
        reach = info[role, slots : slots + 1, :]
        above = jnp.where(key_row >= rows - reach, 0.0, LOW)
        below = jnp.where(key_row < reach, 0.0, LOW)
        for at, (upper, step, there) in enumerate(sides):
            if upper is not None:
                edge = jnp.where(upper, above, below)
            else:
                edge = jnp.where(there, above if step < 0 else below, LOW)
            bias[1 + role * len(sides) + at] = jnp.where(causal, edge, LOW)

    @pl.when(ahead)
    def _():
        landed(info.at[pl.ds(GROUP, GROUP)], asked_sem)
        for role in range(GROUP):
            spread(GROUP + role, base + GROUP + role)

    def attend(query_part, parts):
        scores = []
        most = None
        for pair, shift in parts:
            s = lax.dot_general(query_part, pair[0], (((1,), (1,)), ((), ())),
                                preferred_element_type=jnp.float32) + shift
            most = s if most is None else jnp.maximum(most, s)
            scores.append(s)
        top = jnp.max(most, axis=1, keepdims=True) * SCALE
        total = None
        numerator = None
        for s, (pair, _) in zip(scores, parts):
            w = jnp.exp2(s * SCALE - top)
            total = w if total is None else total + w
            term = jnp.dot(w.astype(jnp.bfloat16), pair[1], preferred_element_type=jnp.float32)
            numerator = term if numerator is None else numerator + term
        return numerator, jnp.sum(total, axis=1, keepdims=True), top

    def distant(at, d):
        return far[at, d : d + 1, :]

    def visit(roles, h):
        for role in roles:
            landed(ask.at[role, h], ask_sem.at[role, h])
            parts = []
            for other in range(GROUP):
                d = role + GROUP - other
                if d <= WIN:
                    parts.append((kv.at[other, h], distant(GROUP + role, d)))
            if role + 1 + GROUP <= WIN:
                pl.when(behind)(lambda: landed(past.at[h], past_sem.at[h]))
                parts.append((past.at[h], distant(GROUP + role, role + 1 + GROUP)))
            numerator, total, top = attend(ask[role, h], parts)
            part[role, h] = (numerator / total).astype(part.dtype)
            level = jnp.broadcast_to(top + jnp.log2(total), (tokens, HD))
            stat[role, h] = jnp.transpose(level)[0:1, :]
            remote(part.at[role, h], back.at[role, h], back_send, back_sem.at[role, h],
                   {"tm": block + GROUP}).start()
            remote(stat.at[role, h], back_stat.at[role, h], stat_send, stat_sem.at[role, h],
                   {"tm": block + GROUP}).start()

    def unit(role, h):
        parts = [(kv.at[role, h], bias[0])]
        for other in range(role):
            parts.append((kv.at[other, h], distant(role, role - other)))

        @pl.when(behind)
        def _():
            landed(back.at[role, h], back_sem.at[role, h])
            landed(back_stat.at[role, h], stat_sem.at[role, h])

        for at, (_, _, there) in enumerate(sides):
            maybe(there, lambda: landed(side.at[at, role, h], side_sem.at[at, role, h]))
        for at in range(len(sides)):
            parts.append((side.at[at, role, h], bias[1 + role * len(sides) + at]))
        found = [attend(qs[role, h], parts)]
        level = jnp.transpose(jnp.broadcast_to(back_stat[role, h], (HD, tokens)))
        peak = level
        for _, _, top in found:
            peak = jnp.maximum(peak, top)
        total = jnp.exp2(level - peak)
        numerator = back[role, h].astype(jnp.float32) * total
        for number, amount, top in found:
            scale = jnp.exp2(top - peak)
            numerator += number * scale
            total += amount * scale
        res[role, h] = (numerator / total).astype(res.dtype)
        place = columns_of(me * share + h)

        @pl.when(me == role)
        def _():
            out_ref[:, place] = res[role, h]

        @pl.when(me != role)
        def _():
            remote(res.at[role, h], out_ref.at[:, place], out_send, out_sem,
                   {"tm": base + role}).start()

    def rest(t):
        def one(n, carry):
            turn = jnp.where(n == 0, across, jnp.where(n == 1, beyond, jnp.where(n == 3, partner, me)))
            for role in range(GROUP):
                pl.when(both(n != 2, t >= 1, turn == role))(lambda: unit(role, t - 1))

            pl.when(both(n == 2, t < share, ahead))(lambda: visit((0,), t))
            return carry

        lax.fori_loop(0, GROUP + 1, one, 0)

    def query_here(h):
        for role in (across, beyond):
            landed(qs.at[role, h], q_sem.at[role, h])
            to_before(role, h)

    def step(t, carry):
        @pl.when(t + 3 < share)
        def _():
            give_across(t + 3, queries_of)

        @pl.when(t + 2 < share)
        def _():
            give_across(t + 2, keys_of)
            settle(t + 2)

        @pl.when(t < share)
        def _():
            for role in (across, beyond):
                landed(kv.at[role, t], kv_sem.at[role, t])
                to_sides(role, t)
                to_next(role, t)

        @pl.when(both(t % 2 == 0, 2 + t // 2 < share))
        def _():
            near_sides(2 + t // 2)

        @pl.when(t < share)
        def _():
            pl.when(t == 0)(lambda: query_here(t))
            pl.when(t + 1 < share)(lambda: query_here(t + 1))
            pl.when(ahead)(lambda: visit(range(1, GROUP), t))
            pl.when(both(behind, jnp.logical_not(ahead)))(lambda: landed(past.at[t], past_sem.at[t]))

        rest(t)

        return carry

    assert share >= 2 and 2 + (share + 1) // 2 >= share
    lax.fori_loop(0, share + 1, step, 0)

    landed(res.at[pl.ds(0, GROUP - 1)], out_sem)
    sent(res.at[pl.ds(0, GROUP - 1)], out_send)
    sent(info.at[pl.ds(0, GROUP - 1)], info_send)
    for at in range(GROUP - 1):
        sent(qs.at[0], in_send.at[at])
        sent(kv.at[0], in_send.at[at])
    for at, (_, _, there) in enumerate(sides):
        maybe(there, lambda: sent(side.at[at], side_send.at[at]))

    @pl.when(ahead)
    def _():
        sent(back, back_send)
        sent(past, past_send)
        sent(back_stat, stat_send)

    @pl.when(behind)
    def _():
        sent(ask, ask_send)
        sent(info.at[pl.ds(0, GROUP)], asked_send)


def local(count, tiles, queries, keys, values, neighbours, halo_rows):
    frames, rows, columns, channels = queries.shape
    tokens = frames * rows * columns
    heads = channels // HD
    share = heads // GROUP
    assert rows == HMAX and count % GROUP == 0 and heads % GROUP == 0
    sides = min(2, tiles - 1)
    flat = (tokens, channels)
    piece = (tokens, HD)
    smem = pl.BlockSpec(memory_space=pltpu.SMEM)
    anywhere = pl.BlockSpec(memory_space=pltpu.HBM)
    dma = pltpu.SemaphoreType.DMA

    def vmem(*size, dtype=jnp.bfloat16):
        return pltpu.VMEM(size, dtype)

    out = pl.pallas_call(
        functools.partial(kernel, count, tiles, (frames, rows, columns)),
        out_shape=pltpu.VMEM(flat, jnp.bfloat16),
        in_specs=[smem, smem, anywhere, anywhere, anywhere],
        out_specs=pl.BlockSpec(memory_space=pltpu.VMEM),
        scratch_shapes=[
            vmem(GROUP, share, *piece),
            vmem(GROUP, share, 2, *piece),
            vmem(max(1, sides), GROUP, share, 2, *piece),
            vmem(share, 2, *piece),
            vmem(GROUP, share, *piece),
            vmem(GROUP, share, *piece),
            vmem(GROUP, share, 1, tokens, dtype=jnp.float32),
            vmem(GROUP, share, *piece),
            vmem(GROUP, share, 1, tokens, dtype=jnp.float32),
            vmem(GROUP, share, *piece),
            vmem(2 * GROUP, ROWS, tokens, dtype=jnp.int32),
            vmem(2 * GROUP, ROWS, tokens, dtype=jnp.float32),
            vmem(1 + GROUP * sides, tokens, tokens, dtype=jnp.float32),
            dma((share,)),
            dma((GROUP, share)),
            dma((GROUP, share)),
            dma((GROUP - 1,)),
            dma((max(1, sides), GROUP, share)),
            dma((max(1, sides),)),
            dma((share,)),
            dma,
            dma((GROUP, share)),
            dma,
            dma((GROUP, share)),
            dma,
            dma((GROUP, share)),
            dma,
            dma,
            dma,
            dma((GROUP,)),
            dma,
            dma,
            dma,
        ],
        compiler_params=pltpu.CompilerParams(
            collective_id=0, has_side_effects=True, vmem_limit_bytes=56 * 1024 * 1024
        ),
    )(
        neighbours.reshape(-1),
        halo_rows.reshape(-1),
        queries.reshape(flat),
        keys.reshape(flat),
        values.reshape(flat),
    )
    return out.reshape(queries.shape)


def solution(mesh):
    return jax.shard_map(
        functools.partial(local, mesh.shape["tm"], mesh.shape["tile"]),
        mesh=mesh,
        in_specs=(
            P("tm", "tile", None, None),
            P("tm", "tile", None, None),
            P("tm", "tile", None, None),
            P("tm", "tile", None),
            P("tm", "tile"),
        ),
        out_specs=P("tm", "tile", None, None),
        check_vma=False,
    )
```

time: 73 us -> 66.9 us (0.916)
  Pallas kernels: 69.1 us -> 63.8 us
  local copies, waits for them, and re-layouts: 2.46 us -> 1.06 us
    pallas_call x1, Pallas kernels: 69.1 us -> 63.8 us  [local(): pl.pallas_call(functools.partial(kernel, count, tiles, (frames, rows, col...]
    unnamed x1, local copies, waits for them, and re-layouts: 2.46 us -> 1.06 us
where the time goes in v2:
time: 66.9 us; the launch traced here: 65.5 us
  Pallas kernels  63.8 us (95%)
  local copies, waits for them, and re-layouts  1.06 us (2%)
    pallas_call x1, Pallas kernels, local(): pl.pallas_call(functools.partial(kernel, count, tiles, (frames, rows, col...  63.8 us

profile of v2, /device:TPU:17, one launch (start us, length us, event | category | flops | bytes accessed | tf_op | source)
XLA Modules:
  0.0 65.5 jit_solution(1794268866767822609)
XLA Ops:
  0.7 63.8 %shard_map.55 = bf16[256,2560]{1,0:T(8,128)(2,1)S(1)} custom-call(s32[3]{0:T(128)} %bitcast.11, s32[1]{0:T(128)} %bitcast.6.halo_ref, bf16[256,2560]{1,0:T(8,128)(2,1)} %bitcast.8, bf16[256,2560]{1,0:T(8,128)(2,1)} %bitcast.9, bf16[256,2560]{1,0:T(8,128)(2,1)} %bitcast.10), custom_call_target="tpu_custom_call" | custom-call | tf_op jit(solution)/shard_map/pallas_call | solution.py:409
  64.5 1.1 %copy.7 = bf16[2,2,64,2560]{3,2,1,0:T(8,128)(2,1)} copy(bf16[2,2,64,2560]{3,2,1,0:T(8,128)(2,1)S(1)} %bitcast.7) | data formatting | bytes 2621440

commit v3 on v2

v3 whole, which is shorter than its diff:
```python
import functools
import math

import jax
import jax.numpy as jnp
from jax import lax
from jax.experimental import pallas as pl
from jax.experimental.pallas import tpu as pltpu
from jax.sharding import PartitionSpec as P

HD = 128
HMAX = 2
WIN = 5
GROUP = 4
FAR, NEAR, MINE = range(3)
Q_SENT, KV_SENT, RES_SENT, INFO_SENT, ASK_SENT, ASKED_SENT, PAST_SENT, BACK_SENT = range(8)
STAT_SENT = BACK_SENT + 2
KINDS = STAT_SENT + 2
ROWS = 8
LOW = -1e30
SCALE = math.log2(math.e) / math.sqrt(HD)


def both(*terms):
    out = terms[0]
    for term in terms[1:]:
        out = jnp.logical_and(out, term)
    return out


def kernel(count, tiles, shape, lists_ref, halo_ref, q_ref, k_ref, v_ref, out_ref,
           qs, kv, side, past, ask, part, stat, back, back_stat, res, info, far, bias,
           send, side_send, local_sem, near_sem, q_sem, kv_sem, side_sem, past_sem, ask_sem,
           back_sem, stat_sem, out_sem, info_sem):
    frames, rows, columns = shape
    tokens = frames * rows * columns
    share = kv.shape[1]
    slots = lists_ref.shape[0]
    block = lax.axis_index("tm")
    tile = lax.axis_index("tile")
    me = block % GROUP
    base = block - me
    partner = me + 1 - 2 * (me % 2)
    across = (me + 2) % GROUP
    beyond = (partner + 2) % GROUP
    behind = block >= GROUP
    ahead = block + GROUP < count
    last = GROUP - 1
    first_chip = me < 2
    early = (me == last).astype(jnp.int32)

    def columns_of(head):
        return pl.ds(pl.multiple_of(head * HD, HD), HD)

    def remote(src, dst, sender, recv, target):
        return pltpu.make_async_remote_copy(
            src_ref=src, dst_ref=dst, send_sem=sender, recv_sem=recv,
            device_id=target, device_id_type=pl.DeviceIdType.MESH,
        )

    def landed(ref, sem):
        remote(ref, ref, send.at[0], sem, {"tm": block}).wait_recv()

    def sent(ref, sem):
        remote(ref, ref, sem, out_sem, {"tm": block}).wait_send()

    if tiles == 2:
        sides = [(tile >= 1, 1 - 2 * tile, None)]
    elif tiles > 2:
        sides = [(None, -1, tile >= 1), (None, 1, tile + 1 < tiles)]
    else:
        sides = []

    def maybe(condition, action):
        if condition is None:
            action()
        else:
            pl.when(condition)(action)

    barrier = pltpu.get_barrier_semaphore()
    expected = jnp.int32(GROUP - 1)

    def greet(target):
        pl.semaphore_signal(barrier, inc=1, device_id=target, device_id_type=pl.DeviceIdType.MESH)

    for role in (across, beyond, partner):
        greet({"tm": base + role})
    for _, step, there in sides:
        maybe(there, lambda: greet({"tile": tile + step}))
        expected += 1 if there is None else there.astype(jnp.int32)
    for there, step in ((behind, -GROUP), (ahead, GROUP)):
        pl.when(there)(lambda: greet({"tm": block + step}))
        expected += there.astype(jnp.int32)

    def spots(h):
        return ((k_ref, kv.at[me, h, 0]), (v_ref, kv.at[me, h, 1]), (q_ref, qs.at[me, h]))

    def fetch(h, carry):
        for ref, spot in spots(h):
            pltpu.make_async_copy(ref.at[:, columns_of(me * share + h)], spot, local_sem).start()
        return carry

    lax.fori_loop(0, share, fetch, 0)

    row = lax.broadcasted_iota(jnp.int32, (ROWS, tokens), 0)
    mine = jnp.where(row == slots, halo_ref[0], -1)
    for n in range(slots):
        mine = jnp.where(row == n, lists_ref[n], mine)
    info[me] = mine

    pl.semaphore_wait(barrier, expected)

    def give(role, h, pairs, sem):
        for ref, spot in pairs:
            kind = Q_SENT if ref is q_ref else KV_SENT
            remote(ref.at[:, columns_of(role * share + h)], spot, send.at[kind], sem,
                   {"tm": base + role}).start()

    def give_keys(h):
        for role in (across, beyond):
            give(role, h, spots(h)[:2], kv_sem.at[early, h])

    def give_queries(h):
        for role in (across, beyond):
            give(role, h, spots(h)[2:], q_sem.at[early, h])

    def to_sides(role, kind, h):
        for at, (_, step, there) in enumerate(sides):
            other = len(sides) - 1 - at
            maybe(there, lambda: remote(
                kv.at[role, h], side.at[other, role, h], side_send.at[at],
                side_sem.at[other, kind, h], {"tile": tile + step}).start())

    def to_next(role, h):
        @pl.when(both(role == last, ahead))
        def _():
            remote(kv.at[role, h], past.at[h], send.at[PAST_SENT], past_sem.at[h],
                   {"tm": block + GROUP}).start()

    def to_before(role, h):
        sem = ask_sem.at[role // last, h]

        @pl.when(behind)
        def _():
            remote(qs.at[role, h], ask.at[role, h], send.at[ASK_SENT], sem,
                   {"tm": block - GROUP}).start()

    def near_z(h):
        for role in (me, partner):
            to_before(role, h)
            to_next(role, h)

    for role in (across, beyond, partner):
        remote(info.at[me], info.at[me], send.at[INFO_SENT], info_sem.at[0],
               {"tm": base + role}).start()
    give_keys(0)
    pltpu.make_async_copy(kv.at[me], kv.at[me], local_sem).wait()
    pltpu.make_async_copy(qs.at[me], qs.at[me], local_sem).wait()
    to_sides(me, MINE, 0)
    for h in range(2):
        give_queries(h)
    give(partner, 0, spots(0), near_sem.at[0])

    def give_rest(h, carry):
        give(partner, h, spots(h), near_sem.at[1])
        return carry

    def give_far(h, carry):
        pl.when(both(me != last, h + 1 < share))(lambda: give_queries(h + 1))
        give_keys(h)
        pl.when(both(me == last, h >= 2))(lambda: give_queries(h))
        return carry

    lax.fori_loop(1, share, give_rest, 0)
    lax.fori_loop(1, share, give_far, 0)
    landed(res.at[pl.ds(0, 3), 0], near_sem.at[0])
    to_sides(partner, NEAR, 0)
    near_z(0)

    landed(info.at[pl.ds(0, GROUP - 1)], info_sem.at[0])

    @pl.when(behind)
    def _():
        remote(info.at[pl.ds(0, GROUP)], info.at[pl.ds(GROUP, GROUP)], send.at[ASKED_SENT],
               info_sem.at[1], {"tm": block - GROUP}).start()

    landed(res.at[pl.ds(0, 3), pl.ds(0, share - 1)], near_sem.at[1])

    def near_sides(h):
        to_sides(partner, NEAR, h)
        to_sides(me, MINE, h)

    near_sides(1)

    @pl.when(jnp.logical_not(behind))
    def _():
        past[...] = jnp.zeros(past.shape, past.dtype)
        back[...] = jnp.zeros(back.shape, back.dtype)
        back_stat[...] = jnp.full(back_stat.shape, LOW, back_stat.dtype)

    for at, (_, _, there) in enumerate(sides):
        if there is not None:

            @pl.when(jnp.logical_not(there))
            def _():
                side[at] = jnp.zeros(side.shape[1:], side.dtype)

    def spread(at, number):
        out = jnp.full((ROWS, tokens), LOW, jnp.float32)
        for d in range(1, WIN + 1):
            wanted = jnp.where(number >= d, number - d, -2)
            hit = info[at, 0:1, :] == wanted
            for n in range(1, slots):
                hit = jnp.logical_or(hit, info[at, n : n + 1, :] == wanted)
            out = jnp.where(jnp.logical_and(row == d, hit), 0.0, out)
        far[at] = out

    query = lax.broadcasted_iota(jnp.int32, (tokens, tokens), 0) // (rows * columns)
    key = lax.broadcasted_iota(jnp.int32, (tokens, tokens), 1)
    causal = key // (rows * columns) <= query
    bias[0] = jnp.where(causal, 0.0, LOW)
    key_row = (lax.broadcasted_iota(jnp.int32, (1, tokens), 1) // columns) % rows
    for role in range(GROUP):
        spread(role, base + role)
        reach = info[role, slots : slots + 1, :]
        above = jnp.where(key_row >= rows - reach, 0.0, LOW)
        below = jnp.where(key_row < reach, 0.0, LOW)
        for at, (upper, step, there) in enumerate(sides):
            if upper is not None:
                edge = jnp.where(upper, above, below)
            else:
                edge = jnp.where(there, above if step < 0 else below, LOW)
            bias[1 + role * len(sides) + at] = jnp.where(causal, edge, LOW)

    @pl.when(ahead)
    def _():
        landed(info.at[pl.ds(GROUP, GROUP)], info_sem.at[1])

        for role in range(GROUP):
            spread(GROUP + role, base + GROUP + role)

    def attend(query_part, parts):
        scores = []
        most = None
        for pair, shift in parts:
            s = lax.dot_general(query_part, pair[0], (((1,), (1,)), ((), ())),
                                preferred_element_type=jnp.float32) + shift
            most = s if most is None else jnp.maximum(most, s)
            scores.append(s)
        top = jnp.max(most, axis=1, keepdims=True) * SCALE
        total = None
        numerator = None
        for s, (pair, _) in zip(scores, parts):
            w = jnp.exp2(s * SCALE - top)
            total = w if total is None else total + w
            term = jnp.dot(w.astype(jnp.bfloat16), pair[1], preferred_element_type=jnp.float32)
            numerator = term if numerator is None else numerator + term
        return numerator, jnp.sum(total, axis=1, keepdims=True), top

    def distant(at, d):
        return far[at, d : d + 1, :]

    def visit(role, h):
        parts = []
        for other in range(GROUP):
            d = role + GROUP - other
            if d <= WIN:
                parts.append((kv.at[other, h], distant(GROUP + role, d)))
        if role + 1 + GROUP <= WIN:
            pl.when(behind)(lambda: landed(past.at[h], past_sem.at[h]))
            parts.append((past.at[h], distant(GROUP + role, role + 1 + GROUP)))
        numerator, total, top = attend(ask[role, h], parts)
        part[role, h] = (numerator / total).astype(part.dtype)
        level = jnp.broadcast_to(top + jnp.log2(total), (tokens, HD))
        stat[role, h] = jnp.transpose(level)[0:1, :]
        kind = role // 2
        remote(part.at[role, h], back.at[role, h], send.at[BACK_SENT + kind], back_sem.at[kind, h],
               {"tm": block + GROUP}).start()
        remote(stat.at[role, h], back_stat.at[role, h], send.at[STAT_SENT + kind],
               stat_sem.at[kind, h], {"tm": block + GROUP}).start()

    two = pl.ds(0, 2)

    def returned(kind, h):
        landed(back.at[two, h], back_sem.at[kind, h])
        landed(back_stat.at[two, h], stat_sem.at[kind, h])

    def sides_here(kind, h):
        roles = {FAR: two, NEAR: partner, MINE: me}[kind]
        for at, (_, _, there) in enumerate(sides):
            maybe(there, lambda: landed(side.at[at, roles, h], side_sem.at[at, kind, h]))

    def unit(role, h, between=None):
        parts = [(kv.at[role, h], bias[0])]
        for other in range(role):
            parts.append((kv.at[other, h], distant(role, role - other)))
        margins = [(side.at[at, role, h], bias[1 + role * len(sides) + at]) for at in range(len(sides))]
        found = []
        if between is not None:
            found.append(attend(qs[role, h], parts))
            parts = []
            between()
        parts += margins
        if parts:
            found.append(attend(qs[role, h], parts))
        level = jnp.transpose(jnp.broadcast_to(back_stat[role, h], (HD, tokens)))
        peak = level
        for _, _, top in found:
            peak = jnp.maximum(peak, top)
        total = jnp.exp2(level - peak)
        numerator = back[role, h].astype(jnp.float32) * total
        for number, amount, top in found:
            scale = jnp.exp2(top - peak)
            numerator += number * scale
            total += amount * scale
        res[role, h] = (numerator / total).astype(res.dtype)
        place = columns_of(me * share + h)

        @pl.when(me == role)
        def _():
            out_ref[:, place] = res[role, h]

        @pl.when(me != role)
        def _():
            remote(res.at[role, h], out_ref.at[:, place], send.at[RES_SENT], out_sem,
                   {"tm": base + role}).start()

    def rest(t):
        h = t - 1

        def one(n, carry):
            turn = jnp.where(n == 0, across, jnp.where(n == 1, beyond, jnp.where(n == 3, partner, me)))
            final = both(n == GROUP, t == share)

            @pl.when(t >= 1)
            def _():
                pl.when(both(n == 0, behind))(lambda: returned(1 - me // 2, h))
                pl.when(both(n == 3, behind))(lambda: returned(me // 2, h))
                pl.when(n == 0)(lambda: sides_here(FAR, h))
                pl.when(n == 3)(lambda: sides_here(NEAR, h))
                pl.when(both(n == GROUP, t < share))(lambda: sides_here(MINE, h))

            for role in range(GROUP):
                pl.when(both(n != 2, t >= 1, turn == role, jnp.logical_not(final)))(
                    lambda: unit(role, h))
                pl.when(both(final, turn == role))(
                    lambda: unit(role, h, lambda: sides_here(MINE, h)))

            pl.when(both(n == 2, t + 1 < share, first_chip))(lambda: early_keys(t + 1))

            @pl.when(both(n == 2, t < share, ahead))
            def _():
                landed(ask.at[last, t], ask_sem.at[1, t])
                visit(last, t)
                visit(0, t)

            return carry

        lax.fori_loop(0, GROUP + 1, one, 0)

    def early_keys(h):
        landed(kv.at[last, h], kv_sem.at[1, h])
        to_next(last, h)
        to_sides(last, FAR, h)

    def late_queries(h):
        landed(qs.at[last, h], q_sem.at[1, h])
        to_before(last, h)

    def keys_here(h):
        @pl.when(first_chip)
        def _():
            landed(kv.at[2, h], kv_sem.at[0, h])
            to_sides(2, FAR, h)

        @pl.when(jnp.logical_not(first_chip))
        def _():
            landed(kv.at[two, h], kv_sem.at[0, h])
            for role in range(2):
                to_sides(role, FAR, h)

    def query_here(h):
        @pl.when(first_chip)
        def _():
            landed(qs.at[2, h], q_sem.at[0, h])
            to_before(2, h)

        @pl.when(jnp.logical_not(first_chip))
        def _():
            landed(qs.at[two, h], q_sem.at[0, h])
            for role in range(2):
                to_before(role, h)

    def step(t, carry):
        @pl.when(t < share)
        def _():
            @pl.when(both(t == 0, first_chip))
            def _():
                early_keys(t)

            keys_here(t)
            pl.when(t + 3 < share)(lambda: near_sides(t + 2))
            pl.when(both(t + 1 == share, share > 2))(lambda: near_sides(t))

            @pl.when(t == 0)
            def _():
                query_here(t)
                pl.when(first_chip)(lambda: late_queries(t))

            @pl.when(t + 1 < share)
            def _():
                query_here(t + 1)
                near_z(t + 1)

            @pl.when(ahead)
            def _():
                landed(ask.at[pl.ds(0, last), t], ask_sem.at[0, t])
                for role in range(1, last):
                    visit(role, t)

            pl.when(both(behind, jnp.logical_not(ahead)))(lambda: landed(past.at[t], past_sem.at[t]))

        rest(t)
        pl.when(both(t + 1 < share, first_chip))(lambda: late_queries(t + 1))
        return carry

    lax.fori_loop(0, share + 1, step, 0)

    peers = pl.ds(0, GROUP - 1)
    landed(res.at[peers], out_sem)
    sent(res.at[peers], send.at[RES_SENT])
    sent(info.at[peers], send.at[INFO_SENT])
    sent(qs.at[peers], send.at[Q_SENT])
    sent(kv.at[peers], send.at[KV_SENT])
    for at, (_, _, there) in enumerate(sides):
        maybe(there, lambda: sent(side.at[at], side_send.at[at]))

    @pl.when(ahead)
    def _():
        sent(past, send.at[PAST_SENT])
        for kind in range(2):
            sent(back.at[two], send.at[BACK_SENT + kind])
            sent(back_stat.at[two], send.at[STAT_SENT + kind])

    @pl.when(behind)
    def _():
        sent(ask, send.at[ASK_SENT])
        sent(info.at[pl.ds(0, GROUP)], send.at[ASKED_SENT])


def local(count, tiles, queries, keys, values, neighbours, halo_rows):
    frames, rows, columns, channels = queries.shape
    tokens = frames * rows * columns
    heads = channels // HD
    share = heads // GROUP
    assert rows == HMAX and count % GROUP == 0 and heads % GROUP == 0
    sides = min(2, tiles - 1)
    flat = (tokens, channels)
    piece = (tokens, HD)
    smem = pl.BlockSpec(memory_space=pltpu.SMEM)
    anywhere = pl.BlockSpec(memory_space=pltpu.HBM)
    dma = pltpu.SemaphoreType.DMA

    def vmem(*size, dtype=jnp.bfloat16):
        return pltpu.VMEM(size, dtype)

    out = pl.pallas_call(
        functools.partial(kernel, count, tiles, (frames, rows, columns)),
        out_shape=pltpu.VMEM(flat, jnp.bfloat16),
        in_specs=[smem, smem, anywhere, anywhere, anywhere],
        out_specs=pl.BlockSpec(memory_space=pltpu.VMEM),
        scratch_shapes=[
            vmem(GROUP, share, *piece),
            vmem(GROUP, share, 2, *piece),
            vmem(max(1, sides), GROUP, share, 2, *piece),
            vmem(share, 2, *piece),
            vmem(GROUP, share, *piece),
            vmem(GROUP, share, *piece),
            vmem(GROUP, share, 1, tokens, dtype=jnp.float32),
            vmem(GROUP, share, *piece),
            vmem(GROUP, share, 1, tokens, dtype=jnp.float32),
            vmem(GROUP, share, *piece),
            vmem(2 * GROUP, ROWS, tokens, dtype=jnp.int32),
            vmem(2 * GROUP, ROWS, tokens, dtype=jnp.float32),
            vmem(1 + GROUP * sides, tokens, tokens, dtype=jnp.float32),
            dma((KINDS,)),
            dma((max(1, sides),)),
            dma,
            dma((2,)),
            dma((2, share)),
            dma((2, share)),
            dma((max(1, sides), 3, share)),
            dma((share,)),
            dma((2, share)),
            dma((2, share)),
            dma((2, share)),
            dma,
            dma((2,)),
        ],
        compiler_params=pltpu.CompilerParams(
            collective_id=0, has_side_effects=True, vmem_limit_bytes=56 * 1024 * 1024
        ),
    )(
        neighbours.reshape(-1),
        halo_rows.reshape(-1),
        queries.reshape(flat),
        keys.reshape(flat),
        values.reshape(flat),
    )
    return out.reshape(queries.shape)


def solution(mesh):
    return jax.shard_map(
        functools.partial(local, mesh.shape["tm"], mesh.shape["tile"]),
        mesh=mesh,
        in_specs=(
            P("tm", "tile", None, None),
            P("tm", "tile", None, None),
            P("tm", "tile", None, None),
            P("tm", "tile", None),
            P("tm", "tile"),
        ),
        out_specs=P("tm", "tile", None, None),
        check_vma=False,
    )
```

time: 66.9 us -> 65.9 us (0.985); the launches traced: 65.5 us -> 65.8 us
  no operation moved by 1% of the time
where the time goes in v3:
time: 65.9 us; the launch traced here: 65.8 us
  Pallas kernels  64.1 us (97%)
  local copies, waits for them, and re-layouts  1.06 us (2%)
  between operations  0.66 us (1%)
    pallas_call x1, Pallas kernels, local(): pl.pallas_call(functools.partial(kernel, count, tiles, (frames, rows, col...  64.1 us

profile of v3, /device:TPU:17, one launch (start us, length us, event | category | flops | bytes accessed | tf_op | source)
XLA Modules:
  0.0 65.8 jit_solution(3465612262513469664)
XLA Ops:
  0.7 64.1 %shard_map.55 = bf16[256,2560]{1,0:T(8,128)(2,1)S(1)} custom-call(s32[3]{0:T(128)} %bitcast.11, s32[1]{0:T(128)} %bitcast.6.halo_ref, bf16[256,2560]{1,0:T(8,128)(2,1)} %bitcast.8, bf16[256,2560]{1,0:T(8,128)(2,1)} %bitcast.9, bf16[256,2560]{1,0:T(8,128)(2,1)} %bitcast.10), custom_call_target="tpu_custom_call" | custom-call | tf_op jit(solution)/shard_map/pallas_call | solution.py:467
  64.7 1.1 %copy.7 = bf16[2,2,64,2560]{3,2,1,0:T(8,128)(2,1)} copy(bf16[2,2,64,2560]{3,2,1,0:T(8,128)(2,1)S(1)} %bitcast.7) | data formatting | bytes 2621440

commit v4 on v3

--- a/solution.py
+++ b/solution.py
@@ -28,14 +28,15 @@
     return out
 
 
-def kernel(count, tiles, shape, lists_ref, halo_ref, q_ref, k_ref, v_ref, out_ref,
+def kernel(count, tiles, shape, lists_hbm, halo_hbm, q_ref, k_ref, v_ref, out_ref,
+           lists_ref, halo_ref,
            qs, kv, side, past, ask, part, stat, back, back_stat, res, info, far, bias,
-           send, side_send, local_sem, near_sem, q_sem, kv_sem, side_sem, past_sem, ask_sem,
+           small_sem, send, side_send, local_sem, near_sem, q_sem, kv_sem, side_sem, past_sem, ask_sem,
            back_sem, stat_sem, out_sem, info_sem):
     frames, rows, columns = shape
     tokens = frames * rows * columns
     share = kv.shape[1]
-    slots = lists_ref.shape[0]
+    slots = lists_ref.shape[2]
     block = lax.axis_index("tm")
     tile = lax.axis_index("tile")
     me = block % GROUP
@@ -47,7 +48,6 @@
     ahead = block + GROUP < count
     last = GROUP - 1
     first_chip = me < 2
-    early = (me == last).astype(jnp.int32)
 
     def columns_of(head):
         return pl.ds(pl.multiple_of(head * HD, HD), HD)
@@ -92,6 +92,9 @@
         pl.when(there)(lambda: greet({"tm": block + step}))
         expected += there.astype(jnp.int32)
 
+    pltpu.make_async_copy(lists_hbm, lists_ref, small_sem.at[0]).start()
+    pltpu.make_async_copy(halo_hbm, halo_ref, small_sem.at[1]).start()
+
     def spots(h):
         return ((k_ref, kv.at[me, h, 0]), (v_ref, kv.at[me, h, 1]), (q_ref, qs.at[me, h]))
 
@@ -102,10 +105,12 @@
 
     lax.fori_loop(0, share, fetch, 0)
 
+    pltpu.make_async_copy(lists_hbm, lists_ref, small_sem.at[0]).wait()
+    pltpu.make_async_copy(halo_hbm, halo_ref, small_sem.at[1]).wait()
     row = lax.broadcasted_iota(jnp.int32, (ROWS, tokens), 0)
-    mine = jnp.where(row == slots, halo_ref[0], -1)
+    mine = jnp.where(row == slots, halo_ref[0, 0, 0], -1)
     for n in range(slots):
-        mine = jnp.where(row == n, lists_ref[n], mine)
+        mine = jnp.where(row == n, lists_ref[0, 0, n], mine)
     info[me] = mine
 
     pl.semaphore_wait(barrier, expected)
@@ -118,11 +123,11 @@
 
     def give_keys(h):
         for role in (across, beyond):
-            give(role, h, spots(h)[:2], kv_sem.at[early, h])
+            give(role, h, spots(h)[:2], kv_sem.at[h])
 
     def give_queries(h):
         for role in (across, beyond):
-            give(role, h, spots(h)[2:], q_sem.at[early, h])
+            give(role, h, spots(h)[2:], q_sem.at[h])
 
     def to_sides(role, kind, h):
         for at, (_, step, there) in enumerate(sides):
@@ -138,11 +143,9 @@
                    {"tm": block + GROUP}).start()
 
     def to_before(role, h):
-        sem = ask_sem.at[role // last, h]
-
         @pl.when(behind)
         def _():
-            remote(qs.at[role, h], ask.at[role, h], send.at[ASK_SENT], sem,
+            remote(qs.at[role, h], ask.at[role, h], send.at[ASK_SENT], ask_sem.at[h],
                    {"tm": block - GROUP}).start()
 
     def near_z(h):
@@ -157,7 +160,7 @@
     pltpu.make_async_copy(kv.at[me], kv.at[me], local_sem).wait()
     pltpu.make_async_copy(qs.at[me], qs.at[me], local_sem).wait()
     to_sides(me, MINE, 0)
-    for h in range(2):
+    for h in range(min(3, share)):
         give_queries(h)
     give(partner, 0, spots(0), near_sem.at[0])
 
@@ -166,9 +169,8 @@
         return carry
 
     def give_far(h, carry):
-        pl.when(both(me != last, h + 1 < share))(lambda: give_queries(h + 1))
         give_keys(h)
-        pl.when(both(me == last, h >= 2))(lambda: give_queries(h))
+        pl.when(h + 2 < share)(lambda: give_queries(h + 2))
         return carry
 
     lax.fori_loop(1, share, give_rest, 0)
@@ -290,29 +292,26 @@
         for at, (_, _, there) in enumerate(sides):
             maybe(there, lambda: landed(side.at[at, roles, h], side_sem.at[at, kind, h]))
 
+    def merge(one, other):
+        peak = jnp.maximum(one[2], other[2])
+        ours, theirs = jnp.exp2(one[2] - peak), jnp.exp2(other[2] - peak)
+        return one[0] * ours + other[0] * theirs, one[1] * ours + other[1] * theirs, peak
+
     def unit(role, h, between=None):
         parts = [(kv.at[role, h], bias[0])]
         for other in range(role):
             parts.append((kv.at[other, h], distant(role, role - other)))
         margins = [(side.at[at, role, h], bias[1 + role * len(sides) + at]) for at in range(len(sides))]
-        found = []
+        level = jnp.transpose(jnp.broadcast_to(back_stat[role, h], (HD, tokens)))
+        so_far = (back[role, h].astype(jnp.float32), 1.0, level)
+        if between is None:
+            parts += margins
+        so_far = merge(so_far, attend(qs[role, h], parts))
         if between is not None:
-            found.append(attend(qs[role, h], parts))
-            parts = []
             between()
-        parts += margins
-        if parts:
-            found.append(attend(qs[role, h], parts))
-        level = jnp.transpose(jnp.broadcast_to(back_stat[role, h], (HD, tokens)))
-        peak = level
-        for _, _, top in found:
-            peak = jnp.maximum(peak, top)
-        total = jnp.exp2(level - peak)
-        numerator = back[role, h].astype(jnp.float32) * total
-        for number, amount, top in found:
-            scale = jnp.exp2(top - peak)
-            numerator += number * scale
-            total += amount * scale
+            if margins:
+                so_far = merge(so_far, attend(qs[role, h], margins))
+        numerator, total, _ = so_far
         res[role, h] = (numerator / total).astype(res.dtype)
         place = columns_of(me * share + h)
 
@@ -329,99 +328,75 @@
         h = t - 1
 
         def one(n, carry):
-            turn = jnp.where(n == 0, across, jnp.where(n == 1, beyond, jnp.where(n == 3, partner, me)))
-            final = both(n == GROUP, t == share)
+            k = jnp.where(n == 2, -1, n - (n > 2).astype(jnp.int32))
+            turn = jnp.where(k == 0, across, jnp.where(k == 1, beyond, jnp.where(k == 2, partner, me)))
+            final = both(k == 3, t == share)
 
             @pl.when(t >= 1)
             def _():
-                pl.when(both(n == 0, behind))(lambda: returned(1 - me // 2, h))
-                pl.when(both(n == 3, behind))(lambda: returned(me // 2, h))
-                pl.when(n == 0)(lambda: sides_here(FAR, h))
-                pl.when(n == 3)(lambda: sides_here(NEAR, h))
-                pl.when(both(n == GROUP, t < share))(lambda: sides_here(MINE, h))
-
+                pl.when(both(k == 0, behind))(lambda: returned(1 - me // 2, h))
+                pl.when(both(k == 2, behind))(lambda: returned(me // 2, h))
+                pl.when(k == 0)(lambda: sides_here(FAR, h))
+                pl.when(k == 2)(lambda: sides_here(NEAR, h))
+                pl.when(both(k == 3, t < share))(lambda: sides_here(MINE, h))
+
+            pl.when(both(k == 3, t + 2 == share))(lambda: keys_here(t + 1))
             for role in range(GROUP):
-                pl.when(both(n != 2, t >= 1, turn == role, jnp.logical_not(final)))(
+                pl.when(both(k >= 0, t >= 1, turn == role, jnp.logical_not(final)))(
                     lambda: unit(role, h))
                 pl.when(both(final, turn == role))(
                     lambda: unit(role, h, lambda: sides_here(MINE, h)))
 
-            pl.when(both(n == 2, t + 1 < share, first_chip))(lambda: early_keys(t + 1))
-
-            @pl.when(both(n == 2, t < share, ahead))
-            def _():
-                landed(ask.at[last, t], ask_sem.at[1, t])
-                visit(last, t)
-                visit(0, t)
-
+            pl.when(both(k < 0, t < share, ahead, first_chip))(lambda: visit(0, t))
+            pl.when(both(k < 0, t < share, ahead, jnp.logical_not(first_chip)))(lambda: visit(last, t))
             return carry
 
         lax.fori_loop(0, GROUP + 1, one, 0)
 
-    def early_keys(h):
-        landed(kv.at[last, h], kv_sem.at[1, h])
-        to_next(last, h)
-        to_sides(last, FAR, h)
-
-    def late_queries(h):
-        landed(qs.at[last, h], q_sem.at[1, h])
-        to_before(last, h)
-
     def keys_here(h):
-        @pl.when(first_chip)
-        def _():
-            landed(kv.at[2, h], kv_sem.at[0, h])
-            to_sides(2, FAR, h)
-
-        @pl.when(jnp.logical_not(first_chip))
-        def _():
-            landed(kv.at[two, h], kv_sem.at[0, h])
-            for role in range(2):
-                to_sides(role, FAR, h)
+        landed(kv.at[two, h], kv_sem.at[h])
+        for role in (across, beyond):
+            to_sides(role, FAR, h)
+            to_next(role, h)
 
     def query_here(h):
-        @pl.when(first_chip)
-        def _():
-            landed(qs.at[2, h], q_sem.at[0, h])
-            to_before(2, h)
-
-        @pl.when(jnp.logical_not(first_chip))
-        def _():
-            landed(qs.at[two, h], q_sem.at[0, h])
-            for role in range(2):
-                to_before(role, h)
+        landed(qs.at[two, h], q_sem.at[h])
+        for role in (across, beyond):
+            to_before(role, h)
 
     def step(t, carry):
         @pl.when(t < share)
         def _():
-            @pl.when(both(t == 0, first_chip))
-            def _():
-                early_keys(t)
-
-            keys_here(t)
-            pl.when(t + 3 < share)(lambda: near_sides(t + 2))
+            pl.when(t + 1 < share)(lambda: keys_here(t))
+            pl.when(t + 3 < share)(lambda: to_sides(partner, NEAR, t + 2))
+            pl.when(both(t == 0, t + 3 < share))(lambda: to_sides(me, MINE, t + 2))
+            pl.when(both(t >= 2, t + 2 < share))(lambda: to_sides(me, MINE, t + 1))
             pl.when(both(t + 1 == share, share > 2))(lambda: near_sides(t))
-
-            @pl.when(t == 0)
-            def _():
-                query_here(t)
-                pl.when(first_chip)(lambda: late_queries(t))
+            pl.when(t == 0)(lambda: query_here(t))
 
             @pl.when(t + 1 < share)
             def _():
                 query_here(t + 1)
-                near_z(t + 1)
+                pl.when(t == 0)(lambda: near_z(t + 1))
+                pl.when(t + 2 < share)(lambda: near_z(t + 2))
 
             @pl.when(ahead)
             def _():
-                landed(ask.at[pl.ds(0, last), t], ask_sem.at[0, t])
-                for role in range(1, last):
-                    visit(role, t)
+                landed(ask.at[:, t], ask_sem.at[t])
+
+                @pl.when(first_chip)
+                def _():
+                    for role in (2, 3, 1):
+                        visit(role, t)
+
+                @pl.when(jnp.logical_not(first_chip))
+                def _():
+                    for role in (1, 0, 2):
+                        visit(role, t)
 
             pl.when(both(behind, jnp.logical_not(ahead)))(lambda: landed(past.at[t], past_sem.at[t]))
 
         rest(t)
-        pl.when(both(t + 1 < share, first_chip))(lambda: late_queries(t + 1))
         return carry
 
     lax.fori_loop(0, share + 1, step, 0)
@@ -457,7 +432,6 @@
     sides = min(2, tiles - 1)
     flat = (tokens, channels)
     piece = (tokens, HD)
-    smem = pl.BlockSpec(memory_space=pltpu.SMEM)
     anywhere = pl.BlockSpec(memory_space=pltpu.HBM)
     dma = pltpu.SemaphoreType.DMA
 
@@ -467,9 +441,11 @@
     out = pl.pallas_call(
         functools.partial(kernel, count, tiles, (frames, rows, columns)),
         out_shape=pltpu.VMEM(flat, jnp.bfloat16),
-        in_specs=[smem, smem, anywhere, anywhere, anywhere],
+        in_specs=[anywhere] * 5,
         out_specs=pl.BlockSpec(memory_space=pltpu.VMEM),
         scratch_shapes=[
+            pltpu.SMEM(neighbours.shape, jnp.int32),
+            pltpu.SMEM((1, 1, 1), jnp.int32),
             vmem(GROUP, share, *piece),
             vmem(GROUP, share, 2, *piece),
             vmem(max(1, sides), GROUP, share, 2, *piece),
@@ -483,15 +459,16 @@
             vmem(2 * GROUP, ROWS, tokens, dtype=jnp.int32),
             vmem(2 * GROUP, ROWS, tokens, dtype=jnp.float32),
             vmem(1 + GROUP * sides, tokens, tokens, dtype=jnp.float32),
+            dma((2,)),
             dma((KINDS,)),
             dma((max(1, sides),)),
             dma,
             dma((2,)),
-            dma((2, share)),
-            dma((2, share)),
+            dma((share,)),
+            dma((share,)),
             dma((max(1, sides), 3, share)),
             dma((share,)),
-            dma((2, share)),
+            dma((share,)),
             dma((2, share)),
             dma((2, share)),
             dma,
@@ -501,8 +478,8 @@
             collective_id=0, has_side_effects=True, vmem_limit_bytes=56 * 1024 * 1024
         ),
     )(
-        neighbours.reshape(-1),
-        halo_rows.reshape(-1),
+        neighbours,
+        halo_rows.reshape(1, 1, 1),
         queries.reshape(flat),
         keys.reshape(flat),
         values.reshape(flat),

time: 65.9 us -> 64.8 us (0.983); the launches traced: 65.8 us -> 63.8 us
  Pallas kernels: 64.1 us -> 62.1 us
    pallas_call x1, Pallas kernels: 64.1 us -> 62.1 us  [local(): pl.pallas_call(functools.partial(kernel, count, tiles, (frames, rows, col...]
where the time goes in v4:
time: 64.8 us; the launch traced here: 63.8 us
  Pallas kernels  62.1 us (96%)
  local copies, waits for them, and re-layouts  1.06 us (2%)
  between operations  0.66 us (1%)
    pallas_call x1, Pallas kernels, local(): pl.pallas_call(functools.partial(kernel, count, tiles, (frames, rows, col...  62.1 us

profile of v4, /device:TPU:17, one launch (start us, length us, event | category | flops | bytes accessed | tf_op | source)
XLA Modules:
  0.0 63.8 jit_solution(3754266839450132879)
XLA Ops:
  0.7 62.1 %shard_map.55 = bf16[256,2560]{1,0:T(8,128)(2,1)S(1)} custom-call(s32[1,1,3]{2,1,0:T(1,128)} %lists_hbm.1, s32[1,1,1]{2,1,0:T(1,128)} %bitcast.5.halo_hbm, bf16[256,2560]{1,0:T(8,128)(2,1)} %bitcast.7, bf16[256,2560]{1,0:T(8,128)(2,1)} %bitcast.8, bf16[256,2560]{1,0:T(8,128)(2,1)} %bitcast.9), custom_call_target="tpu_custom_call" | custom-call | tf_op jit(solution)/shard_map/pallas_call | solution.py:441
  62.8 1.1 %copy.7 = bf16[2,2,64,2560]{3,2,1,0:T(8,128)(2,1)} copy(bf16[2,2,64,2560]{3,2,1,0:T(8,128)(2,1)S(1)} %bitcast.6) | data formatting | bytes 2621440

commit v5 on v4

--- a/solution.py
+++ b/solution.py
@@ -17,7 +17,7 @@
 STAT_SENT = BACK_SENT + 2
 KINDS = STAT_SENT + 2
 ROWS = 8
-LOW = -1e30
+LOW = -1e9
 SCALE = math.log2(math.e) / math.sqrt(HD)
 
 

time: 64.8 us -> 64.8 us (level)
  no operation moved by 1% of the time
where the time goes in v5:
time: 64.8 us; the launch traced here: 63.8 us
  Pallas kernels  62.1 us (96%)
  local copies, waits for them, and re-layouts  1.06 us (2%)
  between operations  0.66 us (1%)
    pallas_call x1, Pallas kernels, local(): pl.pallas_call(functools.partial(kernel, count, tiles, (frames, rows, col...  62.1 us

profile of v5, /device:TPU:17, one launch (start us, length us, event | category | flops | bytes accessed | tf_op | source)
XLA Modules:
  0.0 63.8 jit_solution(5986755002650861651)
XLA Ops:
  0.7 62.1 %shard_map.55 = bf16[256,2560]{1,0:T(8,128)(2,1)S(1)} custom-call(s32[1,1,3]{2,1,0:T(1,128)} %lists_hbm.1, s32[1,1,1]{2,1,0:T(1,128)} %bitcast.5.halo_hbm, bf16[256,2560]{1,0:T(8,128)(2,1)} %bitcast.7, bf16[256,2560]{1,0:T(8,128)(2,1)} %bitcast.8, bf16[256,2560]{1,0:T(8,128)(2,1)} %bitcast.9), custom_call_target="tpu_custom_call" | custom-call | tf_op jit(solution)/shard_map/pallas_call | solution.py:441
  62.8 1.1 %copy.7 = bf16[2,2,64,2560]{3,2,1,0:T(8,128)(2,1)} copy(bf16[2,2,64,2560]{3,2,1,0:T(8,128)(2,1)S(1)} %bitcast.6) | data formatting | bytes 2621440

commit v6 on v5

--- a/solution.py
+++ b/solution.py
@@ -31,7 +31,7 @@
 def kernel(count, tiles, shape, lists_hbm, halo_hbm, q_ref, k_ref, v_ref, out_ref,
            lists_ref, halo_ref,
            qs, kv, side, past, ask, part, stat, back, back_stat, res, info, far, bias,
-           small_sem, send, side_send, local_sem, near_sem, q_sem, kv_sem, side_sem, past_sem, ask_sem,
+           stage, stage_sem, small_sem, send, side_send, local_sem, near_sem, q_sem, kv_sem, side_sem, past_sem, ask_sem,
            back_sem, stat_sem, out_sem, info_sem):
     frames, rows, columns = shape
     tokens = frames * rows * columns
@@ -98,6 +98,10 @@
     def spots(h):
         return ((k_ref, kv.at[me, h, 0]), (v_ref, kv.at[me, h, 1]), (q_ref, qs.at[me, h]))
 
+    for at, role in enumerate((across, beyond)):
+        for i, ref in enumerate((k_ref, v_ref)):
+            pltpu.make_async_copy(ref.at[:, columns_of(role * share)], stage.at[at, i], stage_sem).start()
+
     def fetch(h, carry):
         for ref, spot in spots(h):
             pltpu.make_async_copy(ref.at[:, columns_of(me * share + h)], spot, local_sem).start()
@@ -156,7 +160,9 @@
     for role in (across, beyond, partner):
         remote(info.at[me], info.at[me], send.at[INFO_SENT], info_sem.at[0],
                {"tm": base + role}).start()
-    give_keys(0)
+    pltpu.make_async_copy(stage, stage, stage_sem).wait()
+    for at, role in enumerate((across, beyond)):
+        remote(stage.at[at], kv.at[me, 0], send.at[KV_SENT], kv_sem.at[0], {"tm": base + role}).start()
     pltpu.make_async_copy(kv.at[me], kv.at[me], local_sem).wait()
     pltpu.make_async_copy(qs.at[me], qs.at[me], local_sem).wait()
     to_sides(me, MINE, 0)
@@ -459,6 +465,8 @@
             vmem(2 * GROUP, ROWS, tokens, dtype=jnp.int32),
             vmem(2 * GROUP, ROWS, tokens, dtype=jnp.float32),
             vmem(1 + GROUP * sides, tokens, tokens, dtype=jnp.float32),
+            vmem(2, 2, *piece),
+            dma,
             dma((2,)),
             dma((KINDS,)),
             dma((max(1, sides),)),

time: 64.8 us -> 64.8 us (level)
  no operation moved by 1% of the time
where the time goes in v6:
time: 64.8 us; the launch traced here: 63.8 us
  Pallas kernels  62.1 us (96%)
  local copies, waits for them, and re-layouts  1.06 us (2%)
  between operations  0.66 us (1%)
    pallas_call x1, Pallas kernels, local(): pl.pallas_call(functools.partial(kernel, count, tiles, (frames, rows, col...  62.1 us

profile of v6, /device:TPU:17, one launch (start us, length us, event | category | flops | bytes accessed | tf_op | source)
XLA Modules:
  0.0 63.8 jit_solution(7533315013486786173)
XLA Ops:
  0.7 62.1 %shard_map.55 = bf16[256,2560]{1,0:T(8,128)(2,1)S(1)} custom-call(s32[1,1,3]{2,1,0:T(1,128)} %lists_hbm.1, s32[1,1,1]{2,1,0:T(1,128)} %bitcast.5.halo_hbm, bf16[256,2560]{1,0:T(8,128)(2,1)} %bitcast.7, bf16[256,2560]{1,0:T(8,128)(2,1)} %bitcast.8, bf16[256,2560]{1,0:T(8,128)(2,1)} %bitcast.9), custom_call_target="tpu_custom_call" | custom-call | tf_op jit(solution)/shard_map/pallas_call | solution.py:447
  62.8 1.1 %copy.7 = bf16[2,2,64,2560]{3,2,1,0:T(8,128)(2,1)} copy(bf16[2,2,64,2560]{3,2,1,0:T(8,128)(2,1)S(1)} %bitcast.6) | data formatting | bytes 2621440
